TPU v7x, 32 devices: a whole 2x2x4 slice. The times are simulated.
32 devices in a mesh: groups: 1, blk: 16 (over z, y, x), head: 2 (over core).
Axes of the slice: x: 2, y: 2, z: 4, core: 2. Of those that a mesh axis runs over, the one named last changes fastest.
Arguments:
- queries: bfloat16 [128, 8192], P(('groups', 'blk'), 'head'), may hold values from -6 to 6
- key_cache: bfloat16 [2, 32768, 8, 128], P('groups', 'blk', 'head'), may hold values from -18 to 18
- value_cache: bfloat16 [2, 32768, 8, 128], P('groups', 'blk', 'head'), may hold values from -6 to 6
- lengths: int32 [2], P('groups'), may hold values from 0 to 32704
- residual: bfloat16 [128, 8192], P('groups', 'blk'), may hold values from -6 to 6
- out_weight: bfloat16 [8192, 8192], P('head', 'blk'), may hold values from -0.0625 to 0.0625
- norm_gain: bfloat16 [8192], P('blk'), may hold values from 0.099609375 to 1.8984375
- gate_weight: bfloat16 [8192, 16384], P(None, ('head', 'blk')), may hold values from -0.0625 to 0.0625
- up_weight: bfloat16 [8192, 16384], P(None, ('head', 'blk')), may hold values from -0.0625 to 0.0625
- down_weight: bfloat16 [16384, 8192], P('head', 'blk'), may hold values from -0.046875 to 0.046875
Outputs:
- layer_out: bfloat16 [128, 8192], P('groups', 'blk')
Inputs may be any that keep to these rules, and one draw needn't show every extreme that they name: lengths[b] + 64 <= 32768; the cache holds sequence b's new keys and values at positions lengths[b] to lengths[b] + 63.
All inputs are finite; a program needn't handle non-finite values.
Results may differ from a plain program's by a relative error of at most 0.01.
Values may be sent and summed in bfloat16 or wider, within the bound.
No kernel may reach another device: no remote copies, remote signals or barrier semaphores. Data moves between devices by JAX's collectives and lax.ppermute only.
A program may use at most 128 MiB of HBM per device.

v0:
```python
import jax
import jax.numpy as jnp
from jax import lax
from jax.sharding import PartitionSpec as P

D = 8192
neg_big = -1e30
epsilon = 1e-06


def body(
    queries,
    key_cache,
    value_cache,
    lengths,
    residual,
    out_weight,
    norm_gain,
    gate_weight,
    up_weight,
    down_weight,
):
    blocks = lax.axis_size("blk")
    my_block = lax.axis_index("blk")
    batch, ctx_dev, kv_local, head_dim = key_cache.shape
    rows_dev = queries.shape[0]
    rows_all = rows_dev * blocks
    new_tokens = rows_all // batch
    heads_local = queries.shape[1] // head_dim
    group_size = heads_local // kv_local
    all_queries = lax.all_gather(queries, "blk", axis=0, tiled=True)
    shaped = all_queries.reshape(batch, new_tokens, kv_local, group_size, head_dim)
    scores = jnp.einsum(
        "bqkgd,bckd->bqkgc", shaped, key_cache, preferred_element_type=jnp.float32
    ) * head_dim ** (-0.5)
    query_pos = lengths[:, None] + jnp.arange(new_tokens, dtype=jnp.int32)[None, :]
    key_pos = my_block * ctx_dev + jnp.arange(ctx_dev, dtype=jnp.int32)
    visible = key_pos[None, None, None, None, :] <= query_pos[:, :, None, None, None]
    block_max = jnp.max(jnp.where(visible, scores, neg_big), axis=-1)
    weights = jnp.where(visible, jnp.exp(scores - block_max[..., None]), 0.0)
    block_sum = jnp.sum(weights, axis=-1)
    block_out = jnp.einsum(
        "bqkgc,bckd->bqkgd",
        weights.astype(jnp.bfloat16),
        value_cache,
        preferred_element_type=jnp.float32,
    )
    block_mean = (block_out / jnp.maximum(block_sum, 1.0)[..., None]).astype(jnp.bfloat16)
    row_max = block_max.reshape(rows_all, heads_local)
    row_sum = block_sum.reshape(rows_all, heads_local)
    row_mean = block_mean.reshape(rows_all, heads_local, head_dim)
    got_max, got_sum = (
        lax.all_to_all(row_max[None], "blk", split_axis=1, concat_axis=0, tiled=True),
        lax.all_to_all(row_sum[None], "blk", split_axis=1, concat_axis=0, tiled=True),
    )
    got_mean = lax.all_to_all(row_mean[None], "blk", split_axis=1, concat_axis=0, tiled=True)
    top = jnp.max(got_max, axis=0)
    factor = got_sum * jnp.exp(got_max - top[None])
    total_sum = jnp.sum(factor, axis=0)
    total_out = jnp.sum(got_mean.astype(jnp.float32) * factor[..., None], axis=0)
    attn = (
        (total_out / total_sum[..., None])
        .astype(jnp.bfloat16)
        .reshape(rows_dev, heads_local * head_dim)
    )
    proj_part = jnp.dot(
        lax.all_gather(attn, "blk", axis=0, tiled=True),
        out_weight,
        preferred_element_type=jnp.float32,
    )
    projected = lax.psum(proj_part.astype(jnp.bfloat16), "head").astype(jnp.float32)
    stream = residual.astype(jnp.float32) + projected
    squares = lax.psum(jnp.sum(stream * stream, axis=1), "blk")
    normed = (
        stream * lax.rsqrt(squares / D + epsilon)[:, None] * norm_gain.astype(jnp.float32)[None, :]
    ).astype(jnp.bfloat16)
    piece = lax.all_gather(normed, "blk", axis=1, tiled=True)
    gate = jnp.dot(piece, gate_weight, preferred_element_type=jnp.float32)
    up = jnp.dot(piece, up_weight, preferred_element_type=jnp.float32)
    hidden = (jax.nn.silu(gate) * up).astype(jnp.bfloat16)
    down_part = jnp.dot(
        lax.all_gather(hidden, "blk", axis=1, tiled=True),
        down_weight,
        preferred_element_type=jnp.float32,
    )
    down_total = lax.psum(down_part.astype(jnp.bfloat16), "head").astype(jnp.float32)
    return (stream + down_total).astype(jnp.bfloat16)


def solution(mesh):
    in_specs = (
        P(("groups", "blk"), "head"),
        P("groups", "blk", "head", None),
        P("groups", "blk", "head", None),
        P("groups"),
        P("groups", "blk"),
        P("head", "blk"),
        P("blk"),
        P(None, ("head", "blk")),
        P(None, ("head", "blk")),
        P("head", "blk"),
    )
    out_specs = P("groups", "blk")
    return jax.shard_map(body, mesh=mesh, in_specs=in_specs, out_specs=out_specs, check_vma=False)
```

profile of v0, /device:TPU:0, one launch (start us, length us, event | category | flops | bytes accessed | tf_op | source)
XLA Modules:
  0.0 444.1 jit_solution(5362369163561286765)
XLA Ops:
  8.2 59.7 %all-gather.5.cloned.1.call-done = bf16[128,4096]{1,0:T(8,128)(2,1)} async-done(((bf16[8,4096]{1,0:T(8,128)(2,1)}), bf16[128,4096]{1,0:T(8,128)(2,1)}) %all-gather.5.cloned.1.call-update) | async-done | bytes 1048592 | tf_op jit(solution)/shard_map/all_gather | solution.py:31
  67.9 1.5 copy.45
  69.4 17.1 %fusion = (f32[2,64,4,8]{1,3,2,0:T(8,128)S(1)}, f32[2,4,2048,64,8]{2,3,4,1,0:T(8,128)}) fusion(pred[2,64,2048]{2,1,0:T(8,128)(4,1)S(1)} %broadcast_compare_fusion, bf16[2,64,4,8,128]{4,3,2,1,0:T(8,128)(2,1)S(1)} %bitcast.53, bf16[2,2048,4,128,1]{3,2,1,0,4:T(4,128)(2,1)} %bitcast.55), kind=kOutput, calls=%fused_computation.2 | convolution fusion | flops 2172645376 | bytes 39075840 | tf_op jit(solution)/shard_map/bqkgd,bckd->bqkgc/dot_general | solution.py:33
  86.5 15.1 %fusion.3 = f32[2,64,4,8]{1,3,2,0:T(8,128)S(1)} fusion(f32[2,4,2048,64,8]{2,3,4,1,0:T(8,128)} %get-tuple-element.8, f32[2,64,4,8]{1,3,2,0:T(8,128)S(1)} %get-tuple-element.7, pred[2,64,2048]{2,1,0:T(8,128)(4,1)S(1)} %broadcast_compare_fusion), kind=kLoop, calls=%fused_computation.5 | loop fusion | flops 33550336 | bytes 33849344 | tf_op jit(solution)/shard_map/reduce_sum | solution.py:41
  103.8 4.4 %all-to-all-start.2 = ((f32[16,1,256]{2,1,0:T(1,128)}), f32[16,1,256]{2,1,0:T(1,128)S(1)}, u32[]{:S(2)}, u32[]{:S(2)}) async-start(f32[16,1,256]{2,1,0:T(1,128)} %reshape.82), calls=%async_computation.2 | async-start | bytes 32768 | tf_op jit(solution)/shard_map/all_to_all | solution.py:53
  110.0 5.6 %all-to-all-done.2 = f32[16,1,256]{2,1,0:T(1,128)S(1)} async-done(((f32[16,1,256]{2,1,0:T(1,128)}), f32[16,1,256]{2,1,0:T(1,128)S(1)}, u32[]{:S(2)}, u32[]{:S(2)}) %all-to-all-start.2) | async-done | bytes 16416 | tf_op jit(solution)/shard_map/all_to_all | solution.py:53
  115.6 3.5 all-to-all-start.1
  119.1 15.6 %fusion.12 = bf16[2,64,4,8,128]{4,1,3,2,0:T(8,128)(2,1)S(1)} fusion(bf16[2,2048,4,128,1]{3,2,1,0,4:T(4,128)(2,1)} %bitcast.63, f32[2,4,2048,64,8]{2,3,4,1,0:T(8,128)} %get-tuple-element.8, f32[2,64,4,8]{1,3,2,0:T(8,128)S(1)} %get-tuple-element.7, pred[2,64,2048]{2,1,0:T(8,128)(4,1)S(1)} %broadcast_compare_fusion, f32[2,64,4,8]{1,3,2,0:T(8,128)S(1)} %broadcast_maximum_fusion), kind=kOutput, calls=%fused_computation.15 | convolution fusion | flops 2182086656 | bytes 39092224 | tf_op jit(solution)/shard_map/bqkgc,bckd->bqkgd/dot_general | solution.py:42
  134.8 1.7 copy.33
  136.4 6.9 %all-to-all-start = ((bf16[1,128,32,128]{3,2,0,1:T(8,128)(2,1)}), bf16[1,128,32,128]{3,2,0,1:T(8,128)(2,1)S(1)}, u32[]{:S(2)}, u32[]{:S(2)}) async-start(bf16[1,128,32,128]{3,2,0,1:T(8,128)(2,1)} %bitcast.5), calls=%async_computation | async-start | bytes 2097152 | tf_op jit(solution)/shard_map/all_to_all | solution.py:56
  145.2 19.7 %all-to-all-done = bf16[1,128,32,128]{3,2,0,1:T(8,128)(2,1)S(1)} async-done(((bf16[1,128,32,128]{3,2,0,1:T(8,128)(2,1)}), bf16[1,128,32,128]{3,2,0,1:T(8,128)(2,1)S(1)}, u32[]{:S(2)}, u32[]{:S(2)}) %all-to-all-start) | async-done | bytes 1048608 | tf_op jit(solution)/shard_map/all_to_all | solution.py:56
  166.5 54.4 %all-gather.7.cloned.1.call-done = bf16[128,4096]{1,0:T(8,128)(2,1)} async-done(((bf16[8,4096]{1,0:T(8,128)(2,1)}), bf16[128,4096]{1,0:T(8,128)(2,1)}) %all-gather.7.cloned.1.call-update) | async-done | bytes 1048592 | tf_op jit(solution)/shard_map/all_gather | solution.py:67
  220.9 3.9 convolution_convert_fusion
  224.9 16.8 %all-reduce.3.cloned.1.call-done = bf16[128,512]{1,0:T(8,128)(2,1)} async-done(((bf16[128,512]{1,0:T(8,128)(2,1)}), bf16[128,512]{1,0:T(8,128)(2,1)}) %all-reduce.3.cloned.1.call-update) | async-done | bytes 131088 | tf_op jit(solution)/shard_map/psum | solution.py:71
  241.7 1.0 multiply_reduce_fusion
  242.7 42.0 %psum.22 = f32[128]{0:T(128)S(1)} all-reduce(f32[128]{0:T(128)S(1)} %multiply_reduce_fusion), channel_id=1, replica_groups=mesh['groups'=1,'blk'=16,'head'=2] {'blk'}, use_global_device_ids=true, to_apply=%region_7.8 | all-reduce | flops 128 | bytes 1024 | tf_op jit(solution)/shard_map/psum | solution.py:73
  284.7 1.7 multiply_convert_fusion
  286.5 56.9 %all-gather.9.cloned.1.call-done = bf16[128,8192]{1,0:T(8,128)(2,1)} async-done(((bf16[128,512]{1,0:T(8,128)(2,1)}), bf16[128,8192]{1,0:T(8,128)(2,1)}) %all-gather.9.cloned.1.call-update) | async-done | bytes 2097168 | tf_op jit(solution)/shard_map/all_gather | solution.py:77
  343.3 5.4 %fusion.23 = f32[128,512]{1,0:T(8,128)S(1)} fusion(bf16[128,8192]{1,0:T(8,128)(2,1)} %all-gather.9.cloned.1.call-done, bf16[8192,512]{1,0:T(8,128)(2,1)} %param.17), kind=kOutput, calls=%fused_computation.37 | convolution fusion | flops 1073741824 | bytes 10747904 | tf_op jit(solution)/shard_map/dot_general | solution.py:78
  348.7 5.4 %fusion.17 = bf16[128,512]{1,0:T(8,128)(2,1)} fusion(bf16[128,8192]{1,0:T(8,128)(2,1)S(1)} %copy-done, bf16[8192,512]{1,0:T(8,128)(2,1)} %param.18, f32[128,512]{1,0:T(8,128)S(1)} %fusion.23), kind=kOutput, calls=%fused_computation.17 | convolution fusion | flops 1074135040 | bytes 10878976 | tf_op jit(solution)/shard_map/dot_general | solution.py:79
  354.3 59.2 %all-gather.11.cloned.1.call-done = bf16[128,8192]{1,0:T(8,128)(2,1)} async-done(((bf16[128,512]{1,0:T(8,128)(2,1)}), bf16[128,8192]{1,0:T(8,128)(2,1)}) %all-gather.11.cloned.1.call-update) | async-done | bytes 2097168 | tf_op jit(solution)/shard_map/all_gather | solution.py:82
  413.4 5.9 %convolution_convert_fusion.1 = bf16[128,512]{1,0:T(8,128)(2,1)} fusion(bf16[128,8192]{1,0:T(8,128)(2,1)} %all-gather.11.cloned.1.call-done, bf16[8192,512]{1,0:T(8,128)(2,1)} %param.19), kind=kOutput, calls=%fused_computation.19 | convolution fusion | flops 1073807360 | bytes 10616832 | tf_op jit(solution)/shard_map/dot_general | solution.py:81
  419.4 16.2 %all-reduce.5.cloned.1.call-done = bf16[128,512]{1,0:T(8,128)(2,1)} async-done(((bf16[128,512]{1,0:T(8,128)(2,1)}), bf16[128,512]{1,0:T(8,128)(2,1)}) %all-reduce.5.cloned.1.call-update) | async-done | bytes 131088 | tf_op jit(solution)/shard_map/psum | solution.py:86
  435.6 1.6 add_convert_fusion
  (47 shorter events, 9.2 us)
Async XLA Ops:
  6.5 61.4 %all-gather.5.cloned.1.call-start = ((), (), s32[]{:S(2)}) async-start(), calls=%async_computation.3 | async-start | bytes 1114112 | tf_op jit(solution)/shard_map/all_gather | solution.py:31
  103.8 11.8 %all-to-all-start.2 = ((f32[16,1,256]{2,1,0:T(1,128)}), f32[16,1,256]{2,1,0:T(1,128)S(1)}, u32[]{:S(2)}, u32[]{:S(2)}) async-start(f32[16,1,256]{2,1,0:T(1,128)} %reshape.82), calls=%async_computation.2 | async-start | bytes 32768 | tf_op jit(solution)/shard_map/all_to_all | solution.py:53
  115.6 20.8 %all-to-all-start.1 = ((f32[16,1,256]{2,1,0:T(1,128)}), f32[16,1,256]{2,1,0:T(1,128)S(1)}, u32[]{:S(2)}, u32[]{:S(2)}) async-start(f32[16,1,256]{2,1,0:T(1,128)} %reshape.80), calls=%async_computation.1 | async-start | bytes 32768 | tf_op jit(solution)/shard_map/all_to_all | solution.py:54
  134.7 90.1 %copy-start.3 = (bf16[512]{0:T(512)(128)(2,1)S(1)}, bf16[512]{0:T(512)(128)(2,1)}, u32[]{:S(2)}) copy-start(bf16[512]{0:T(512)(128)(2,1)} %param.16) | copy-start | bytes 3076
  134.7 106.9 %copy-start.1 = (bf16[128,512]{1,0:T(8,128)(2,1)S(1)}, bf16[128,512]{1,0:T(8,128)(2,1)}, u32[]{:S(2)}) copy-start(bf16[128,512]{1,0:T(8,128)(2,1)} %param.14) | copy-start | bytes 393220
  136.4 28.5 %all-to-all-start = ((bf16[1,128,32,128]{3,2,0,1:T(8,128)(2,1)}), bf16[1,128,32,128]{3,2,0,1:T(8,128)(2,1)S(1)}, u32[]{:S(2)}, u32[]{:S(2)}) async-start(bf16[1,128,32,128]{3,2,0,1:T(8,128)(2,1)} %bitcast.5), calls=%async_computation | async-start | bytes 2097152 | tf_op jit(solution)/shard_map/all_to_all | solution.py:56
  143.3 77.6 %all-gather.7.cloned.1.call-start = ((), (), s32[]{:S(2)}) async-start(), calls=%async_computation.4 | async-start | bytes 1114112 | tf_op jit(solution)/shard_map/all_gather | solution.py:67
  166.4 75.2 %all-reduce.3.cloned.1.call-start = ((), (), s32[]{:S(2)}) async-start(), calls=%async_computation.5 | async-start | bytes 262144 | tf_op jit(solution)/shard_map/psum | solution.py:71
  224.8 118.5 %all-gather.9.cloned.1.call-start = ((), (), s32[]{:S(2)}) async-start(), calls=%async_computation.6 | async-start | bytes 2228224 | tf_op jit(solution)/shard_map/all_gather | solution.py:77
  286.4 127.0 %all-gather.11.cloned.1.call-start = ((), (), s32[]{:S(2)}) async-start(), calls=%async_computation.7 | async-start | bytes 2228224 | tf_op jit(solution)/shard_map/all_gather | solution.py:82
  343.3 5.4 %copy-start = (bf16[128,8192]{1,0:T(8,128)(2,1)S(1)}, bf16[128,8192]{1,0:T(8,128)(2,1)}, u32[]{:S(2)}) copy-start(bf16[128,8192]{1,0:T(8,128)(2,1)} %all-gather.9.cloned.1.call-done) | copy-start | bytes 6291460
  354.2 81.4 %copy-start.2 = (bf16[128,512]{1,0:T(8,128)(2,1)S(1)}, bf16[128,512]{1,0:T(8,128)(2,1)}, u32[]{:S(2)}) copy-start(bf16[128,512]{1,0:T(8,128)(2,1)} %all-reduce.3.cloned.1.call-done) | copy-start | bytes 393220
  354.2 81.4 %all-reduce.5.cloned.1.call-start = ((), (), s32[]{:S(2)}) async-start(), calls=%async_computation.8 | async-start | bytes 262144 | tf_op jit(solution)/shard_map/psum | solution.py:86
Sparse Core Ops, SparseCore 0:
  10.1 57.7 all-gather.4
  166.6 54.2 all-gather.6
  224.9 16.7 all-reduce.2
  286.5 56.7 all-gather.8
  354.3 59.0 all-gather.10
  419.5 16.0 all-reduce.4
where the time goes:
time: 445 us; the launch traced here: 444 us
  waiting for transfers between devices  289 us (65%)
  matrix products  53.4 us (12%)
  blocking collectives  42 us (9%)
  other arithmetic  24 us (5%)
  starting transfers between devices  15.2 us (3%)
  between operations  13.7 us (3%)
  local copies, waits for them, and re-layouts  6.46 us (1%)
    all_gather x1, waiting for transfers between devices, body(): all_queries = lax.all_gather(queries, 'blk', axis=0, tiled=True)  59.7 us
    all_gather x1, waiting for transfers between devices, body(): lax.all_gather(hidden, 'blk', axis=1, tiled=True)  59.2 us
    all_gather x1, waiting for transfers between devices, body(): piece = lax.all_gather(normed, 'blk', axis=1, tiled=True)  56.9 us
    all_gather x1, waiting for transfers between devices, body(): lax.all_gather(attn, 'blk', axis=0, tiled=True)  54.4 us
    psum x1, blocking collectives, body(): squares = lax.psum(jnp.sum(stream * stream, axis=1), 'blk')  42 us
    all_to_all x1, waiting for transfers between devices, body(): lax.all_to_all(row_mean[None], 'blk', split_axis=1, concat_axis=0, tiled=...  19.7 us
    dot_general x1, matrix products, body(): jnp.einsum('bqkgd,bckd->bqkgc', shaped, key_cache, preferred_element_type...  17.1 us
    psum x1, waiting for transfers between devices, body(): lax.psum(proj_part.astype(jnp.bfloat16), 'head').astype(jnp.float32)  16.8 us
  transfers between devices with their start and end apart: 9, of which 8 were waited for; matrix products, arithmetic and copies ran while one was open for 5% of the time, Pallas kernels for 0%

commit v1 on v0

--- a/solution.py
+++ b/solution.py
@@ -6,6 +6,28 @@
 D = 8192
 neg_big = -1e30
 epsilon = 1e-06
+
+
+def joined_along(blocks, dim):
+    blocks = jnp.moveaxis(blocks, 0, dim)
+    dims = blocks.shape
+    return blocks.reshape(*dims[:dim], dims[dim] * dims[dim + 1], *dims[dim + 2 :])
+
+
+def grow_blocks(shard, axis):
+    peers = lax.axis_size(axis)
+    blocks = shard[None]
+    for level in range(peers.bit_length() - 1):
+        bit = 1 << level
+        other = lax.ppermute(blocks, axis, [(i, i ^ bit) for i in range(peers)])
+        both = jnp.stack([blocks, other])
+        upper = lax.axis_index(axis) >> level & 1
+        blocks = jnp.where(upper == 0, both, both[::-1]).reshape(-1, *shard.shape)
+    return blocks
+
+
+def collect(value, axis, dim):
+    return joined_along(grow_blocks(value, axis), dim)
 
 
 def body(
@@ -63,11 +85,7 @@
         .astype(jnp.bfloat16)
         .reshape(rows_dev, heads_local * head_dim)
     )
-    proj_part = jnp.dot(
-        lax.all_gather(attn, "blk", axis=0, tiled=True),
-        out_weight,
-        preferred_element_type=jnp.float32,
-    )
+    proj_part = jnp.dot(collect(attn, "blk", 0), out_weight, preferred_element_type=jnp.float32)
     projected = lax.psum(proj_part.astype(jnp.bfloat16), "head").astype(jnp.float32)
     stream = residual.astype(jnp.float32) + projected
     squares = lax.psum(jnp.sum(stream * stream, axis=1), "blk")

time: 445 us -> 426 us (0.957)
  waiting for transfers between devices: 289 us -> 266 us
  starting transfers between devices: 15.2 us -> 19.7 us
    all_gather x1 -> x0, waiting for transfers between devices: 54.4 us -> none  [body(): lax.all_gather(attn, 'blk', axis=0, tiled=True)]
    ppermute x0 -> x4, waiting for transfers between devices: none -> 31.3 us  [grow_blocks(): other = lax.ppermute(blocks, axis, [(i, i ^ bit) for i in range(peers)])]
    ppermute x0 -> x4, starting transfers between devices: none -> 4.54 us  [grow_blocks(): other = lax.ppermute(blocks, axis, [(i, i ^ bit) for i in range(peers)])]
  transfers between devices with their start and end apart: 9 -> 12, of which waited for: 8 -> 11; matrix products, arithmetic and copies ran while one was open for 5% -> 5% of each run, Pallas kernels for 0% -> 0%
where the time goes in v1:
time: 426 us; the launch traced here: 425 us
  waiting for transfers between devices  266 us (62%)
  matrix products  53.1 us (12%)
  blocking collectives  42 us (10%)
  other arithmetic  24.6 us (6%)
  starting transfers between devices  19.7 us (5%)
  between operations  13.4 us (3%)
  local copies, waits for them, and re-layouts  5.87 us (1%)
    all_gather x1, waiting for transfers between devices, body(): all_queries = lax.all_gather(queries, 'blk', axis=0, tiled=True)  59.7 us
    all_gather x1, waiting for transfers between devices, body(): lax.all_gather(hidden, 'blk', axis=1, tiled=True)  59.2 us
    all_gather x1, waiting for transfers between devices, body(): piece = lax.all_gather(normed, 'blk', axis=1, tiled=True)  56.9 us
    psum x1, blocking collectives, body(): squares = lax.psum(jnp.sum(stream * stream, axis=1), 'blk')  42 us
    ppermute x4, waiting for transfers between devices, grow_blocks(): other = lax.ppermute(blocks, axis, [(i, i ^ bit) for i in range(peers)])  31.3 us
    all_to_all x1, waiting for transfers between devices, body(): lax.all_to_all(row_mean[None], 'blk', split_axis=1, concat_axis=0, tiled=...  19.7 us
    psum x1, waiting for transfers between devices, body(): lax.psum(proj_part.astype(jnp.bfloat16), 'head').astype(jnp.float32)  17.1 us
    dot_general x1, matrix products, body(): jnp.einsum('bqkgd,bckd->bqkgc', shaped, key_cache, preferred_element_type...  17.1 us
  transfers between devices with their start and end apart: 12, of which 11 were waited for; matrix products, arithmetic and copies ran while one was open for 5% of the time, Pallas kernels for 0%

profile of v1, /device:TPU:0, one launch (start us, length us, event | category | flops | bytes accessed | tf_op | source)
XLA Modules:
  0.0 425.1 jit_solution(14439871669304791414)
XLA Ops:
  8.2 59.7 %all-gather.4.cloned.1.call-done = bf16[128,4096]{1,0:T(8,128)(2,1)} async-done(((bf16[8,4096]{1,0:T(8,128)(2,1)}), bf16[128,4096]{1,0:T(8,128)(2,1)}) %all-gather.4.cloned.1.call-update) | async-done | bytes 1048592 | tf_op jit(solution)/shard_map/all_gather | solution.py:53
  69.4 17.1 %fusion = (f32[2,64,4,8]{1,3,2,0:T(8,128)S(1)}, f32[2,4,2048,64,8]{2,3,4,1,0:T(8,128)}) fusion(pred[2,64,2048]{2,1,0:T(8,128)(4,1)S(1)} %broadcast_compare_fusion, bf16[2,64,4,8,128]{4,3,2,1,0:T(8,128)(2,1)S(1)} %bitcast.61, bf16[2,2048,4,128,1]{3,2,1,0,4:T(4,128)(2,1)} %bitcast.64), kind=kOutput, calls=%fused_computation.2 | convolution fusion | flops 2172645376 | bytes 39075840 | tf_op jit(solution)/shard_map/bqkgd,bckd->bqkgc/dot_general | solution.py:55
  86.5 15.1 %fusion.3 = f32[2,64,4,8]{1,3,2,0:T(8,128)S(1)} fusion(f32[2,4,2048,64,8]{2,3,4,1,0:T(8,128)} %get-tuple-element.10, f32[2,64,4,8]{1,3,2,0:T(8,128)S(1)} %get-tuple-element.9, pred[2,64,2048]{2,1,0:T(8,128)(4,1)S(1)} %broadcast_compare_fusion), kind=kLoop, calls=%fused_computation.5 | loop fusion | flops 33550336 | bytes 33849344 | tf_op jit(solution)/shard_map/reduce_sum | solution.py:63
  103.8 4.4 %all-to-all-start.2 = ((f32[16,1,256]{2,1,0:T(1,128)}), f32[16,1,256]{2,1,0:T(1,128)S(1)}, u32[]{:S(2)}, u32[]{:S(2)}) async-start(f32[16,1,256]{2,1,0:T(1,128)} %reshape.137), calls=%async_computation.2 | async-start | bytes 32768 | tf_op jit(solution)/shard_map/all_to_all | solution.py:75
  110.0 5.6 %all-to-all-done.2 = f32[16,1,256]{2,1,0:T(1,128)S(1)} async-done(((f32[16,1,256]{2,1,0:T(1,128)}), f32[16,1,256]{2,1,0:T(1,128)S(1)}, u32[]{:S(2)}, u32[]{:S(2)}) %all-to-all-start.2) | async-done | bytes 16416 | tf_op jit(solution)/shard_map/all_to_all | solution.py:75
  115.6 3.5 all-to-all-start.1
  119.1 15.6 %fusion.12 = bf16[2,64,4,8,128]{4,1,3,2,0:T(8,128)(2,1)S(1)} fusion(bf16[2,2048,4,128,1]{3,2,1,0,4:T(4,128)(2,1)} %bitcast.79, f32[2,4,2048,64,8]{2,3,4,1,0:T(8,128)} %get-tuple-element.10, f32[2,64,4,8]{1,3,2,0:T(8,128)S(1)} %get-tuple-element.9, pred[2,64,2048]{2,1,0:T(8,128)(4,1)S(1)} %broadcast_compare_fusion, f32[2,64,4,8]{1,3,2,0:T(8,128)S(1)} %broadcast_maximum_fusion), kind=kOutput, calls=%fused_computation.15 | convolution fusion | flops 2182086656 | bytes 39092224 | tf_op jit(solution)/shard_map/bqkgc,bckd->bqkgd/dot_general | solution.py:64
  134.7 1.7 copy.33
  136.4 6.9 %all-to-all-start = ((bf16[1,128,32,128]{3,2,0,1:T(8,128)(2,1)}), bf16[1,128,32,128]{3,2,0,1:T(8,128)(2,1)S(1)}, u32[]{:S(2)}, u32[]{:S(2)}) async-start(bf16[1,128,32,128]{3,2,0,1:T(8,128)(2,1)} %bitcast.5), calls=%async_computation | async-start | bytes 2097152 | tf_op jit(solution)/shard_map/all_to_all | solution.py:78
  145.2 19.7 %all-to-all-done = bf16[1,128,32,128]{3,2,0,1:T(8,128)(2,1)S(1)} async-done(((bf16[1,128,32,128]{3,2,0,1:T(8,128)(2,1)}), bf16[1,128,32,128]{3,2,0,1:T(8,128)(2,1)S(1)}, u32[]{:S(2)}, u32[]{:S(2)}) %all-to-all-start) | async-done | bytes 1048608 | tf_op jit(solution)/shard_map/all_to_all | solution.py:78
  166.4 3.7 collective-permute-done
  171.5 3.6 collective-permute-done.1
  175.3 2.0 collective-permute-start.2
  177.3 7.9 %collective-permute-done.2 = bf16[4,8,4096]{2,1,0:T(8,128)(2,1)S(1)} collective-permute-done((bf16[4,8,4096]{2,1,0:T(8,128)(2,1)S(1)}, bf16[4,8,4096]{2,1,0:T(8,128)(2,1)S(1)}, u32[]{:S(2)}, u32[]{:S(2)}) %collective-permute-start.2) | collective-permute-done | bytes 262176 | tf_op jit(solution)/shard_map/ppermute | solution.py:22
  185.9 16.1 %collective-permute-done.3 = bf16[8,8,4096]{2,1,0:T(8,128)(2,1)S(1)} collective-permute-done((bf16[8,8,4096]{2,1,0:T(8,128)(2,1)S(1)}, bf16[8,8,4096]{2,1,0:T(8,128)(2,1)S(1)}, u32[]{:S(2)}, u32[]{:S(2)}) %collective-permute-start.3) | collective-permute-done | bytes 524320 | tf_op jit(solution)/shard_map/ppermute | solution.py:22
  202.2 3.6 convolution_convert_fusion
  205.9 17.1 %all-reduce.3.cloned.1.call-done = bf16[128,512]{1,0:T(8,128)(2,1)} async-done(((bf16[128,512]{1,0:T(8,128)(2,1)}), bf16[128,512]{1,0:T(8,128)(2,1)}) %all-reduce.3.cloned.1.call-update) | async-done | bytes 131088 | tf_op jit(solution)/shard_map/psum | solution.py:89
  224.1 42.0 %psum.22 = f32[128]{0:T(128)S(1)} all-reduce(f32[128]{0:T(128)S(1)} %multiply_reduce_fusion), channel_id=1, replica_groups=mesh['groups'=1,'blk'=16,'head'=2] {'blk'}, use_global_device_ids=true, to_apply=%region_7.8 | all-reduce | flops 128 | bytes 1024 | tf_op jit(solution)/shard_map/psum | solution.py:91
  267.8 56.9 %all-gather.6.cloned.1.call-done = bf16[128,8192]{1,0:T(8,128)(2,1)} async-done(((bf16[128,512]{1,0:T(8,128)(2,1)}), bf16[128,8192]{1,0:T(8,128)(2,1)}) %all-gather.6.cloned.1.call-update) | async-done | bytes 2097168 | tf_op jit(solution)/shard_map/all_gather | solution.py:95
  324.7 5.4 %fusion.24 = f32[128,512]{1,0:T(8,128)S(1)} fusion(bf16[128,8192]{1,0:T(8,128)(2,1)} %all-gather.6.cloned.1.call-done, bf16[8192,512]{1,0:T(8,128)(2,1)} %param.17), kind=kOutput, calls=%fused_computation.45 | convolution fusion | flops 1073741824 | bytes 10747904 | tf_op jit(solution)/shard_map/dot_general | solution.py:96
  330.1 5.4 %fusion.17 = bf16[128,512]{1,0:T(8,128)(2,1)} fusion(bf16[128,8192]{1,0:T(8,128)(2,1)S(1)} %copy-done, bf16[8192,512]{1,0:T(8,128)(2,1)} %param.18, f32[128,512]{1,0:T(8,128)S(1)} %fusion.24), kind=kOutput, calls=%fused_computation.18 | convolution fusion | flops 1074135040 | bytes 10878976 | tf_op jit(solution)/shard_map/dot_general | solution.py:97
  335.6 59.2 %all-gather.8.cloned.1.call-done = bf16[128,8192]{1,0:T(8,128)(2,1)} async-done(((bf16[128,512]{1,0:T(8,128)(2,1)}), bf16[128,8192]{1,0:T(8,128)(2,1)}) %all-gather.8.cloned.1.call-update) | async-done | bytes 2097168 | tf_op jit(solution)/shard_map/all_gather | solution.py:100
  394.8 5.9 %convolution_convert_fusion.1 = bf16[128,512]{1,0:T(8,128)(2,1)} fusion(bf16[128,8192]{1,0:T(8,128)(2,1)} %all-gather.8.cloned.1.call-done, bf16[8192,512]{1,0:T(8,128)(2,1)} %param.19), kind=kOutput, calls=%fused_computation.20 | convolution fusion | flops 1073807360 | bytes 10616832 | tf_op jit(solution)/shard_map/dot_general | solution.py:99
  400.7 16.2 %all-reduce.5.cloned.1.call-done = bf16[128,512]{1,0:T(8,128)(2,1)} async-done(((bf16[128,512]{1,0:T(8,128)(2,1)}), bf16[128,512]{1,0:T(8,128)(2,1)}) %all-reduce.5.cloned.1.call-update) | async-done | bytes 131088 | tf_op jit(solution)/shard_map/psum | solution.py:104
  (61 shorter events, 17.3 us)
Async XLA Ops:
  6.5 61.4 %all-gather.4.cloned.1.call-start = ((), (), s32[]{:S(2)}) async-start(), calls=%async_computation.3 | async-start | bytes 1114112 | tf_op jit(solution)/shard_map/all_gather | solution.py:53
  103.8 11.8 %all-to-all-start.2 = ((f32[16,1,256]{2,1,0:T(1,128)}), f32[16,1,256]{2,1,0:T(1,128)S(1)}, u32[]{:S(2)}, u32[]{:S(2)}) async-start(f32[16,1,256]{2,1,0:T(1,128)} %reshape.137), calls=%async_computation.2 | async-start | bytes 32768 | tf_op jit(solution)/shard_map/all_to_all | solution.py:75
  115.6 20.8 %all-to-all-start.1 = ((f32[16,1,256]{2,1,0:T(1,128)}), f32[16,1,256]{2,1,0:T(1,128)S(1)}, u32[]{:S(2)}, u32[]{:S(2)}) async-start(f32[16,1,256]{2,1,0:T(1,128)} %reshape.135), calls=%async_computation.1 | async-start | bytes 32768 | tf_op jit(solution)/shard_map/all_to_all | solution.py:76
  136.4 28.5 %all-to-all-start = ((bf16[1,128,32,128]{3,2,0,1:T(8,128)(2,1)}), bf16[1,128,32,128]{3,2,0,1:T(8,128)(2,1)S(1)}, u32[]{:S(2)}, u32[]{:S(2)}) async-start(bf16[1,128,32,128]{3,2,0,1:T(8,128)(2,1)} %bitcast.5), calls=%async_computation | async-start | bytes 2097152 | tf_op jit(solution)/shard_map/all_to_all | solution.py:78
  143.3 62.6 %copy-start.3 = (bf16[512]{0:T(512)(128)(2,1)S(1)}, bf16[512]{0:T(512)(128)(2,1)}, u32[]{:S(2)}) copy-start(bf16[512]{0:T(512)(128)(2,1)} %param.16) | copy-start | bytes 3076
  143.3 79.7 %copy-start.1 = (bf16[128,512]{1,0:T(8,128)(2,1)S(1)}, bf16[128,512]{1,0:T(8,128)(2,1)}, u32[]{:S(2)}) copy-start(bf16[128,512]{1,0:T(8,128)(2,1)} %param.14) | copy-start | bytes 393220
  143.3 79.7 %all-reduce.3.cloned.1.call-start = ((), (), s32[]{:S(2)}) async-start(), calls=%async_computation.4 | async-start | bytes 262144 | tf_op jit(solution)/shard_map/psum | solution.py:89
  165.8 4.3 %collective-permute-start = (bf16[1,8,4096]{2,1,0:T(8,128)(2,1)S(1)}, bf16[1,8,4096]{2,1,0:T(8,128)(2,1)S(1)}, u32[]{:S(2)}, u32[]{:S(2)}) collective-permute-start(bf16[1,8,4096]{2,1,0:T(8,128)(2,1)S(1)} %convert_element_type.72), channel_id=1, source_target_pairs={{0,2},{2,0},{4,6},{6,4},{8,10},{10,8},{12,14},{14,12},{16,18},{18,... | collective-permute-start | bytes 196616 | tf_op jit(solution)/shard_map/ppermute | solution.py:22
  170.2 5.0 %collective-permute-start.1 = (bf16[2,8,4096]{2,1,0:T(8,128)(2,1)S(1)}, bf16[2,8,4096]{2,1,0:T(8,128)(2,1)S(1)}, u32[]{:S(2)}, u32[]{:S(2)}) collective-permute-start(bf16[2,8,4096]{2,1,0:T(8,128)(2,1)S(1)} %get-tuple-element.8), channel_id=1, source_target_pairs={{0,4},{2,6},{4,0},{6,2},{8,12},{10,14},{12,8},{14,10},{16,20},{18,... | collective-permute-start | bytes 393224 | tf_op jit(solution)/shard_map/ppermute | solution.py:22
  175.3 9.9 %collective-permute-start.2 = (bf16[4,8,4096]{2,1,0:T(8,128)(2,1)S(1)}, bf16[4,8,4096]{2,1,0:T(8,128)(2,1)S(1)}, u32[]{:S(2)}, u32[]{:S(2)}) collective-permute-start(bf16[4,8,4096]{2,1,0:T(8,128)(2,1)S(1)} %bitcast.68), channel_id=1, source_target_pairs={{0,8},{2,10},{4,12},{6,14},{8,0},{10,2},{12,4},{14,6},{16,24},{18,... | collective-permute-start | bytes 786440 | tf_op jit(solution)/shard_map/ppermute | solution.py:22
  185.4 16.6 %collective-permute-start.3 = (bf16[8,8,4096]{2,1,0:T(8,128)(2,1)S(1)}, bf16[8,8,4096]{2,1,0:T(8,128)(2,1)S(1)}, u32[]{:S(2)}, u32[]{:S(2)}) collective-permute-start(bf16[8,8,4096]{2,1,0:T(8,128)(2,1)S(1)} %bitcast.65), channel_id=1, source_target_pairs={{0,16},{2,18},{4,20},{6,22},{8,24},{10,26},{12,28},{14,30},{16,0},... | collective-permute-start | bytes 1572872 | tf_op jit(solution)/shard_map/ppermute | solution.py:22
  205.9 118.8 %all-gather.6.cloned.1.call-start = ((), (), s32[]{:S(2)}) async-start(), calls=%async_computation.5 | async-start | bytes 2228224 | tf_op jit(solution)/shard_map/all_gather | solution.py:95
  267.8 127.0 %all-gather.8.cloned.1.call-start = ((), (), s32[]{:S(2)}) async-start(), calls=%async_computation.6 | async-start | bytes 2228224 | tf_op jit(solution)/shard_map/all_gather | solution.py:100
  324.7 5.4 %copy-start = (bf16[128,8192]{1,0:T(8,128)(2,1)S(1)}, bf16[128,8192]{1,0:T(8,128)(2,1)}, u32[]{:S(2)}) copy-start(bf16[128,8192]{1,0:T(8,128)(2,1)} %all-gather.6.cloned.1.call-done) | copy-start | bytes 6291460
  335.5 81.4 %copy-start.2 = (bf16[128,512]{1,0:T(8,128)(2,1)S(1)}, bf16[128,512]{1,0:T(8,128)(2,1)}, u32[]{:S(2)}) copy-start(bf16[128,512]{1,0:T(8,128)(2,1)} %all-reduce.3.cloned.1.call-done) | copy-start | bytes 393220
  335.6 81.4 %all-reduce.5.cloned.1.call-start = ((), (), s32[]{:S(2)}) async-start(), calls=%async_computation.7 | async-start | bytes 262144 | tf_op jit(solution)/shard_map/psum | solution.py:104
Sparse Core Ops, SparseCore 0:
  10.1 57.7 all-gather.3
  206.0 17.0 all-reduce.2
  267.9 56.7 all-gather.5
  335.7 59.0 all-gather.7
  400.9 16.0 all-reduce.4
